TPU v7x, 128 devices: a whole 4x4x4 slice. The times are simulated.
128 devices in a mesh: section: 8 (over x, y_lo), seq: 16 (over z, y_hi, core).
Axes of the slice: x: 4, y: 4 (y_hi: 2, y_lo: 2; y = y_hi * 2 + y_lo), z: 4, core: 2. Of those that a mesh axis runs over, the one named last changes fastest.
Arguments:
- queries: bfloat16 [8, 2048, 4096], P('section', 'seq'), may hold values from -500 to 500
- keys: bfloat16 [8, 2048, 512], P('section', 'seq'), may hold values from -6 to 6
- values: bfloat16 [8, 2048, 512], P('section', 'seq'), may hold values from -6 to 6
- out_grad: bfloat16 [8, 2048, 4096], P('section', 'seq'), may hold values from -6 to 6
- documents: int32 [8, 2048], P('section'), may hold values from 0 to 3, never falling along the last dimension, each value on 1 to 1024 neighbouring positions
- query_weight: bfloat16 [8, 4096, 4096], P('section', 'seq'), may hold values from -0.09375 to 0.09375
- key_weight: bfloat16 [8, 512, 4096], P('section'), may hold values from -0.125 to 0.125
- value_weight: bfloat16 [8, 512, 4096], P('section'), may hold values from -0.125 to 0.125
Outputs:
- upstream: bfloat16 [8, 2048, 4096], P('section', 'seq')
Inputs may be any that keep to these rules, and one draw needn't show every extreme that they name: `documents`: each section's document ids never fall along its tokens.
All inputs are finite; a program needn't handle non-finite values.
Results may differ from a plain program's by a relative error of at most 0.0058.
Values may be sent and summed in bfloat16 or wider, within the bound.
A program may use at most 192 MiB of HBM per device.

v0:
```python
import math

import jax
import jax.numpy as jnp
from jax import lax
from jax.experimental import pallas as pl
from jax.experimental.pallas import tpu as pltpu
from jax.sharding import PartitionSpec as P

HD = 128
ROWS = 128
GW = 1024
D = 4096
NC = 8
CW = D // NC
W_EARLY = 7
EARLY = 3
SLOTS = 8
ORDER = ('w3', 'p0', 'm0', 'core', 'p3', 'p1', 'm1', 'w4', 'p2', 'p4', 'w5', 'p5', 'm2', 'w6', 'p6', 'ysum', 'm3', 'm4', 'm5', 'dkv', 'w7', 'f0', 'f1', 'f2', 'f3', 'p7', 'm6', 'f4', 'f5', 'm7', 'f6', 'f7')
WIN = 9
SCALE = 1.0 / math.sqrt(HD)
NEG = -1e30
MESH = pl.DeviceIdType.MESH
F32 = jnp.float32
BF16 = jnp.bfloat16


def remote(src, dst, send, recv, device):
    return pltpu.make_async_remote_copy(
        src_ref=src, dst_ref=dst, send_sem=send, recv_sem=recv, device_id=device, device_id_type=MESH
    )


def kernel(
    q_ref, k_ref, v_ref, o_ref, doc_ref, w_ref, wk_ref, wv_ref,
    out_ref,
    qs, os_, kv, start, p_s, ds_s, dk, dv, dq, w8, wkv, half_s, half_r, full_s, full_r, part, own,
    dkv_s, dkv_c, dkv_o, dkv_t, dkv_p, dkv_i, fin,
    loc, kvz_s, kvz_r, kvy_s, kvy_r, kvc_s, kvc_r, qo_s, qo_r,
    w0_s, w0_r, wy_s, wy_r, wc_s, wc_r, wf_s, wf_r, ra_s, ra_r, rb_s, rb_r, dc_s, dc_r, dd_s, dd_r, hop_s, hop_r,
):
    sec = lax.axis_index("section")
    seq = lax.axis_index("seq")
    z = seq // 4
    y = lax.rem(seq // 2, 2)
    c = lax.rem(seq, 2)
    yc = y * 2 + c

    def dev(zz, yy, cc):
        return (sec, zz * 4 + yy * 2 + cc)

    def zoff(d):
        return lax.rem(z + d, 4)

    core = dev(z, y, 1 - c)
    ypart = dev(z, 1 - y, c)

    own_q = pltpu.make_async_copy(q_ref.at[:, pl.ds(pl.multiple_of(z * GW, GW), GW)], qs.at[z], loc.at[0])
    own_o = pltpu.make_async_copy(o_ref.at[:, pl.ds(pl.multiple_of(z * GW, GW), GW)], os_.at[z], loc.at[1])
    own_k = pltpu.make_async_copy(
        k_ref.at[:, pl.ds(pl.multiple_of(z * HD, HD), HD)], kv.at[z + 2, yc, :, 0:HD], loc.at[2]
    )
    own_v = pltpu.make_async_copy(
        v_ref.at[:, pl.ds(pl.multiple_of(z * HD, HD), HD)], kv.at[z + 2, yc, :, HD : 2 * HD], loc.at[3]
    )
    own_w = pltpu.make_async_copy(w_ref, w8.at[yc], loc.at[4])
    own_wk = pltpu.make_async_copy(wk_ref, wkv.at[:, 0], loc.at[5])
    own_wv = pltpu.make_async_copy(wv_ref, wkv.at[:, 1], loc.at[6])
    barrier = pltpu.get_barrier_semaphore()
    for partner in (dev(zoff(1), y, c), dev(zoff(2), y, c), dev(zoff(3), y, c), ypart, core):
        pl.semaphore_signal(barrier, inc=1, device_id=partner, device_id_type=MESH)

    @pl.when(sec > 0)
    def _():
        pl.semaphore_signal(barrier, inc=1, device_id=(sec - 1, seq), device_id_type=MESH)

    @pl.when(sec < 7)
    def _():
        pl.semaphore_signal(barrier, inc=1, device_id=(sec + 1, seq), device_id_type=MESH)

    for copy in (own_k, own_v, own_q, own_o, own_w, own_wk, own_wv):
        copy.start()
    doc = doc_ref[...]
    first = jnp.zeros_like(doc)
    for value in (1, 2, 3):
        before = jnp.sum((doc < value).astype(F32), axis=1, keepdims=True).astype(jnp.int32)
        first = jnp.where(doc == value, before, first)
    start[...] = first
    kv[0:2] = jnp.zeros((2, 4, ROWS, 2 * HD), BF16)
    dk[...] = jnp.zeros_like(dk)
    dv[...] = jnp.zeros_like(dv)
    own_k.wait()
    own_v.wait()
    with jax.named_scope("barrier"):
        pl.semaphore_wait(barrier, 5 + jnp.where(sec > 0, 1, 0) + jnp.where(sec < 7, 1, 0))

    kv_copies = []
    for d in (1, 3, 2):
        zd = zoff(d)
        cols = pl.ds(pl.multiple_of(zd * HD, HD), HD)
        kv_copies.append(
            (
                remote(k_ref.at[:, cols], kv.at[z + 2, yc, :, 0:HD], kvz_s.at[0, d], kvz_r.at[0, d], dev(zd, y, c)),
                remote(
                    v_ref.at[:, cols], kv.at[z + 2, yc, :, HD : 2 * HD], kvz_s.at[1, d], kvz_r.at[1, d], dev(zd, y, c)
                ),
            )
        )
    for pair in kv_copies:
        pair[0].start()
        pair[1].start()

    def kv_y(d):
        zs = lax.rem(z + 4 - d, 4) + 2
        return remote(kv.at[zs, yc], kv.at[zs, yc], kvy_s.at[d], kvy_r.at[d], ypart)

    def kv_y_in(d):
        zs = lax.rem(z + 4 - d, 4) + 2
        at = (1 - y) * 2 + c
        return remote(kv.at[zs, at], kv.at[zs, at], kvy_s.at[d], kvy_r.at[d], ypart)

    def kv_c(i, d):
        zs = lax.rem(z + 4 - d, 4) + 2
        at = yc if i == 0 else (1 - y) * 2 + c
        return remote(kv.at[zs, at], kv.at[zs, at], kvc_s.at[i, d], kvc_r.at[i, d], core)

    def kv_c_in(i, d):
        zs = lax.rem(z + 4 - d, 4) + 2
        at = (y if i == 0 else 1 - y) * 2 + 1 - c
        return remote(kv.at[zs, at], kv.at[zs, at], kvc_s.at[i, d], kvc_r.at[i, d], core)

    def w_y0(i):
        cols = pl.ds(i * (CW // 2), CW // 2)
        return remote(w_ref.at[:, cols], w8.at[yc, :, cols], w0_s.at[i], w0_r.at[i], ypart)

    def w_y0_in(i):
        cols = pl.ds(i * (CW // 2), CW // 2)
        at = (1 - y) * 2 + c
        return remote(w_ref.at[:, cols], w8.at[at, :, cols], w0_s.at[i], w0_r.at[i], ypart)

    def w_y(n):
        cols = pl.ds(n * CW, CW)
        return remote(w_ref.at[:, cols], w8.at[yc, :, cols], wy_s.at[n], wy_r.at[n], ypart)

    def w_y_in(n):
        cols = pl.ds(n * CW, CW)
        at = (1 - y) * 2 + c
        return remote(w_ref.at[:, cols], w8.at[at, :, cols], wy_s.at[n], wy_r.at[n], ypart)

    w_core = remote(w_ref, w8.at[yc], wc_s.at[0], wc_r.at[0], core)

    def w_fwd(n):
        cols = pl.ds(n * CW, CW)
        at = (1 - y) * 2 + c
        return remote(w8.at[at, :, cols], w8.at[at, :, cols], wf_s.at[n], wf_r.at[n], core)

    def w_fwd_in(n):
        cols = pl.ds(n * CW, CW)
        at = (1 - y) * 2 + 1 - c
        return remote(w8.at[at, :, cols], w8.at[at, :, cols], wf_s.at[n], wf_r.at[n], core)

    qo_copies = {}
    for d in (1, 3, 2):
        zd = zoff(d)
        cols = pl.ds(pl.multiple_of(zd * GW, GW), GW)
        qo_copies[d] = (
            remote(q_ref.at[:, cols], qs.at[z], qo_s.at[0, d], qo_r.at[0, d], dev(zd, y, c)),
            remote(o_ref.at[:, cols], os_.at[z], qo_s.at[1, d], qo_r.at[1, d], dev(zd, y, c)),
        )

    kv_y(0).start()
    kv_c(0, 0).start()
    w_y0(0).start()
    with jax.named_scope("kvz"):
        for d in (1, 3, 2):
            zs = lax.rem(z + 4 - d, 4)
            remote(k_ref.at[:, 0:HD], kv.at[zs + 2, yc, :, 0:HD], kvz_s.at[0, d], kvz_r.at[0, d], core).wait_recv()
            remote(
                v_ref.at[:, 0:HD], kv.at[zs + 2, yc, :, HD : 2 * HD], kvz_s.at[1, d], kvz_r.at[1, d], core
            ).wait_recv()
            kv_y(d).start()
            kv_c(0, d).start()
    for d in (1, 3, 2):
        for copy in qo_copies[d]:
            copy.start()
    w_y0(1).start()
    for n in range(1, W_EARLY):
        w_y(n).start()
    with jax.named_scope("kvy"):
        for d in (0, 1, 3, 2):
            kv_y_in(d).wait_recv()
            kv_c(1, d).start()
    w_core.start()
    with jax.named_scope("kvc"):
        for i in range(2):
            for d in range(4):
                kv_c_in(i, d).wait_recv()

    kv_rows = kv.reshape(24 * ROWS, 2 * HD)
    w_rows = w8.reshape(GW, D)
    up, down = dev(zoff(1), y, c), dev(zoff(3), y, c)
    far = pl.ds(pl.multiple_of(zoff(2) * ROWS, ROWS), ROWS)

    def half(i, n):
        return remote(half_s.at[i, n], half_r.at[i, n], ra_s.at[i, n], ra_r.at[i, n], up if i == 0 else down)

    def full(i, n):
        return remote(full_s.at[i, n], full_r.at[i, n], rb_s.at[i, n], rb_r.at[i, n], up if i == 0 else down)

    def forward(n, carry):
        w_y_in(n).wait_recv()
        w_fwd(n).start()
        return carry

    def forward_early(n, carry):
        @pl.when(n == 0)
        def _():
            w_y0_in(0).wait_recv()
            w_y0_in(1).wait_recv()

        @pl.when(n > 0)
        def _():
            w_y_in(n).wait_recv()

        w_fwd(n).start()
        return carry

    def early(n, carry):
        cols = pl.ds(pl.multiple_of(n * CW, CW), CW)
        w_fwd_in(n).wait_recv()
        res = jnp.dot(dq[far, :], w_rows[:, cols], preferred_element_type=F32).astype(BF16)
        for i in range(2):
            half_s[i, n] = res[:, i * (CW // 2) : (i + 1) * (CW // 2)]
            half(i, n).start()
        return carry

    def attend(i, carry):
        d = jnp.where(i == 2, 3, jnp.where(i == 3, 2, i))
        zb = lax.rem(z + 4 - d, 4)
        lo, hi = jnp.where(i == 3, 0, 0), jnp.where(i == 3, 3, 0)

        with jax.named_scope("qowait"):

            @pl.when(d == 0)
            def _():
                own_q.wait()
                own_o.wait()

            @pl.when(d > 0)
            def _():
                remote(q_ref.at[:, 0:GW], qs.at[zb], qo_s.at[0, d], qo_r.at[0, d], core).wait_recv()
                remote(o_ref.at[:, 0:GW], os_.at[zb], qo_s.at[1, d], qo_r.at[1, d], core).wait_recv()

        @pl.when(i == 1)
        def _():
            own_w.wait()
            w_core.wait()

        with jax.named_scope("forward"):
            lax.fori_loop(lo, hi, forward_early, 0)
        block = zb * 4 + yc
        at = pl.multiple_of(block * ROWS, ROWS)
        k_win = kv_rows[pl.ds(at, WIN * ROWS), 0:HD]
        base = (block - 8) * ROWS
        lower = start[:, pl.ds(at, ROWS)] - base
        lower = jnp.concatenate([lower, lower], axis=1)

        def heads(hp, carry):
            cols = pl.ds(pl.multiple_of(hp * 2 * HD, 2 * HD), 2 * HD)
            q2 = qs[zb, :, cols]
            q2 = jnp.concatenate([q2[:, 0:HD], q2[:, HD:]], axis=0)
            o2 = os_[zb, :, cols]
            o2 = jnp.concatenate([o2[:, 0:HD], o2[:, HD:]], axis=0)
            v_win = kv_rows[pl.ds(at, WIN * ROWS), HD : 2 * HD]
            k_win = kv_rows[pl.ds(at, WIN * ROWS), 0:HD]
            nt = (((1,), (1,)), ((), ()))
            s = lax.dot_general(k_win, q2, nt, preferred_element_type=F32)
            key = lax.broadcasted_iota(jnp.int32, (8 * ROWS, 2 * ROWS), 0)
            s_a = jnp.where(key >= lower, s[: 8 * ROWS], NEG)
            key = lax.broadcasted_iota(jnp.int32, (ROWS, 2 * ROWS), 0)
            row = lax.broadcasted_iota(jnp.int32, (ROWS, 2 * ROWS), 1)
            row = jnp.where(row >= ROWS, row - ROWS, row)
            s_b = jnp.where((key + 8 * ROWS >= lower) & (key <= row), s[8 * ROWS :], NEG)
            s = jnp.concatenate([s_a, s_b], axis=0)
            top = jnp.max(s, axis=0, keepdims=True)
            e = jnp.exp2((s - top) * (SCALE * math.log2(math.e)))
            inv = 1.0 / jnp.sum(e, axis=0, keepdims=True)
            dp = lax.dot_general(v_win, o2, nt, preferred_element_type=F32)
            delta = jnp.sum(e * dp, axis=0, keepdims=True) * inv
            p_s[:, cols] = (e * inv).astype(BF16)
            ds_s[:, cols] = (e * (dp - delta) * (inv * SCALE)).astype(BF16)
            return carry

        with jax.named_scope("heads"):
            lax.fori_loop(0, 4, heads, 0, unroll=4)
        with jax.named_scope("grads"):
            qb = qs[zb]
            ob = os_[zb]
            qb = jnp.concatenate([qb[:, h * HD : (h + 1) * HD] for h in range(8)], axis=0)
            ob = jnp.concatenate([ob[:, h * HD : (h + 1) * HD] for h in range(8)], axis=0)
            win = pl.ds(at, WIN * ROWS)
            dv[win, :] += jnp.dot(p_s[...], ob, preferred_element_type=F32)
            dk[win, :] += jnp.dot(ds_s[...], qb, preferred_element_type=F32)
            dqt = lax.dot_general(k_win, ds_s[...], (((0,), (0,)), ((), ())), preferred_element_type=F32)
            for h in range(8):
                dq[pl.ds(pl.multiple_of(zb * ROWS, ROWS), ROWS), h * HD : (h + 1) * HD] = dqt[
                    :, h * HD : (h + 1) * HD
                ].T.astype(BF16)
        with jax.named_scope("early"):
            lax.fori_loop(lo, hi, early, 0)
        return carry

    lax.fori_loop(0, 4, attend, 0)

    def blocks(b, carry):
        rows = pl.ds(pl.multiple_of((b * 2 + 1 - c + 8) * ROWS, ROWS), ROWS)
        at = lax.rem(b, 2)
        dkv_s[at, b // 2, :, 0:HD] = dk[rows, :].astype(BF16)
        dkv_s[at, b // 2, :, HD : 2 * HD] = dv[rows, :].astype(BF16)
        return carry

    lax.fori_loop(0, 8, blocks, 0)
    dkv_core = remote(dkv_s, dkv_c, dc_s.at[0], dc_r.at[0], core)
    dkv_core.start()

    def dd_y(i):
        return remote(dkv_o.at[1 - y], dkv_t, dd_s.at[0], dd_r.at[0], ypart)

    def dd_z(d):
        zz = zoff(d)
        return remote(dkv_p.at[zz], dkv_i.at[z], dd_s.at[d], dd_r.at[d], dev(zz, y, c))

    def product(n):
        cols = slice(n * CW, (n + 1) * CW)
        slot = n % SLOTS
        if n >= EARLY:
            with jax.named_scope("prodwait"):
                w_fwd_in(n).wait_recv()
        with jax.named_scope("proddot"):
            part[slot] = jnp.dot(dq[...], w_rows[:, cols], preferred_element_type=F32)
            own[:, cols] = part[slot, pl.ds(pl.multiple_of(z * ROWS, ROWS), ROWS), :]
            if n >= EARLY:
                for i in range(2):
                    half_s[i, n] = part[slot, far, i * (CW // 2) : (i + 1) * (CW // 2)].astype(BF16)
                for i in range(2):
                    half(i, n).start()

    def merge(n):
        slot = n % SLOTS
        for i in range(2):
            with jax.named_scope("mergewait"):
                half(i, n).wait_recv()
            rows = pl.ds(pl.multiple_of(zoff(1 if i == 0 else 3) * ROWS, ROWS), ROWS)
            mine = slice(0, CW // 2) if i == 0 else slice(CW // 2, CW)
            rest = slice(CW // 2, CW) if i == 0 else slice(0, CW // 2)
            full_s[i, n, :, mine] = (part[slot, rows, mine] + half_r[i, n].astype(F32)).astype(BF16)
            full_s[i, n, :, rest] = part[slot, rows, rest].astype(BF16)
            full(i, n).start()

    def hop(n):
        cols = pl.ds(n * CW, CW)
        return remote(fin.at[:, cols], out_ref.at[:, cols], hop_s.at[n], hop_r.at[n], (jnp.maximum(sec - 1, 0), seq))

    def finish(n):
        cols = slice(n * CW, (n + 1) * CW)
        with jax.named_scope("findot"):
            dkv = jnp.concatenate([dkv_i[zz] for zz in range(4)], axis=1)
            total = own[:, cols] + jnp.dot(dkv, wkv.reshape(GW, D)[:, cols], preferred_element_type=F32)
        with jax.named_scope("finwait"):
            full(0, n).wait_recv()
            full(1, n).wait_recv()
        total = total + full_r[0, n].astype(F32) + full_r[1, n].astype(F32)
        fin[:, cols] = total.astype(BF16)

        @pl.when(sec > 0)
        def _():
            hop(n).start()

    def dkv_core_sum():
        dkv_core.wait_recv()
        for yy in range(2):

            def add(zz, carry):
                rows = pl.ds(pl.multiple_of((zz * 4 + yy * 2 + c + 8) * ROWS, ROWS), ROWS)
                dkv_o[yy, zz, :, 0:HD] = (dk[rows, :] + dkv_c[yy, zz, :, 0:HD].astype(F32)).astype(BF16)
                dkv_o[yy, zz, :, HD : 2 * HD] = (dv[rows, :] + dkv_c[yy, zz, :, HD : 2 * HD].astype(F32)).astype(BF16)
                return carry

            lax.fori_loop(0, 4, add, 0)
        dd_y(0).start()
        for n in range(W_EARLY, NC):
            w_y(n).start()

    def dkv_y_sum():
        dd_y(0).wait_recv()

        def add(zz, carry):
            dkv_p[zz] = (dkv_o[y, zz].astype(F32) + dkv_t[zz].astype(F32)).astype(BF16)
            return carry

        lax.fori_loop(0, 4, add, 0)
        for d in (2, 1, 3):
            dd_z(d).start()
        dkv_i[z] = dkv_p[z]
        own_wk.wait()
        own_wv.wait()

    def dkv_arrived():
        for d in (2, 1, 3):
            zs = lax.rem(z + 4 - d, 4)
            remote(dkv_p.at[zs], dkv_i.at[zs], dd_s.at[d], dd_r.at[d], core).wait_recv()

    steps = {"p": product, "m": merge, "f": finish, "w": lambda n: forward(n, 0)}
    for step in ORDER:
        if step == "core":
            with jax.named_scope("dkvcore"):
                dkv_core_sum()
        elif step == "ysum":
            with jax.named_scope("ddywait"):
                dkv_y_sum()
        elif step == "dkv":
            with jax.named_scope("ddwait"):
                dkv_arrived()
        else:
            with jax.named_scope(step):
                steps[step[0]](int(step[1:]))

    @pl.when(sec == 7)
    def _():
        out_ref[...] = jnp.zeros_like(out_ref)

    with jax.named_scope("drain"):
        for pair in kv_copies:
            pair[0].wait_send()
            pair[1].wait_send()
        for d in range(4):
            kv_y(d).wait_send()
            kv_c(0, d).wait_send()
            kv_c(1, d).wait_send()
        for d in (1, 2, 3):
            for copy in qo_copies[d]:
                copy.wait_send()
        dkv_core.wait_send()
        dd_y(0).wait_send()
        for d in (1, 2, 3):
            dd_z(d).wait_send()

        def drain(n, carry):
            @pl.when(n > 0)
            def _():
                w_y(n).wait_send()

            w_fwd(n).wait_send()
            for i in range(2):
                half(i, n).wait_send()
                full(i, n).wait_send()

            @pl.when(sec > 0)
            def _():
                hop(n).wait_send()

            @pl.when(sec < 7)
            def _():
                hop(n).wait_recv()

            return carry

        w_y0(0).wait_send()
        w_y0(1).wait_send()
        lax.fori_loop(0, NC, drain, 0)


def body(queries, keys, values, out_grad, documents, query_weight, key_weight, value_weight):
    hbm = pl.BlockSpec(memory_space=pltpu.MemorySpace.HBM)
    vmem = pl.BlockSpec(memory_space=pltpu.VMEM)
    dma = pltpu.SemaphoreType.DMA
    scratch = [
        pltpu.VMEM((4, ROWS, GW), BF16),
        pltpu.VMEM((4, ROWS, GW), BF16),
        pltpu.VMEM((6, 4, ROWS, 2 * HD), BF16),
        pltpu.VMEM((1, 2048), jnp.int32),
        pltpu.VMEM((WIN * ROWS, GW), BF16),
        pltpu.VMEM((WIN * ROWS, GW), BF16),
        pltpu.VMEM((24 * ROWS, HD), F32),
        pltpu.VMEM((24 * ROWS, HD), F32),
        pltpu.VMEM((4 * ROWS, GW), BF16),
        pltpu.VMEM((4, 256, D), BF16),
        pltpu.VMEM((4, 2, HD, D), BF16),
        pltpu.VMEM((2, NC, ROWS, CW // 2), BF16),
        pltpu.VMEM((2, NC, ROWS, CW // 2), BF16),
        pltpu.VMEM((2, NC, ROWS, CW), BF16),
        pltpu.VMEM((2, NC, ROWS, CW), BF16),
        pltpu.VMEM((SLOTS, 4 * ROWS, CW), F32),
        pltpu.VMEM((ROWS, D), F32),
        pltpu.VMEM((2, 4, ROWS, 2 * HD), BF16),
        pltpu.VMEM((2, 4, ROWS, 2 * HD), BF16),
        pltpu.VMEM((2, 4, ROWS, 2 * HD), BF16),
        pltpu.VMEM((4, ROWS, 2 * HD), BF16),
        pltpu.VMEM((4, ROWS, 2 * HD), BF16),
        pltpu.VMEM((4, ROWS, 2 * HD), BF16),
        pltpu.VMEM((ROWS, D), BF16),
        dma((7,)),
        dma((2, 4)), dma((2, 4)),
        dma((4,)), dma((4,)),
        dma((2, 4)), dma((2, 4)),
        dma((2, 4)), dma((2, 4)),
        dma((2,)), dma((2,)),
        dma((NC,)), dma((NC,)),
        dma((1,)), dma((1,)),
        dma((NC,)), dma((NC,)),
        dma((2, NC)), dma((2, NC)),
        dma((2, NC)), dma((2, NC)),
        dma((1,)), dma((1,)),
        dma((4,)), dma((4,)),
        dma((NC,)), dma((NC,)),
    ]
    out = pl.pallas_call(
        kernel,
        out_shape=pltpu.VMEM((ROWS, D), BF16),
        in_specs=[hbm, hbm, hbm, hbm, vmem, hbm, hbm, hbm],
        out_specs=vmem,
        scratch_shapes=scratch,
        compiler_params=pltpu.CompilerParams(
            collective_id=0, has_side_effects=True, vmem_limit_bytes=60817408
        ),
    )(
        queries[0],
        keys[0],
        values[0],
        out_grad[0],
        documents,
        query_weight[0],
        key_weight[0].reshape(4, HD, D),
        value_weight[0].reshape(4, HD, D),
    )
    return out[None]


def solution(mesh):
    in_specs = (
        P("section", "seq", None),
        P("section", "seq", None),
        P("section", "seq", None),
        P("section", "seq", None),
        P("section", None),
        P("section", "seq", None),
        P("section", None, None),
        P("section", None, None),
    )
    out_specs = P("section", "seq", None)
    return jax.shard_map(body, mesh=mesh, in_specs=in_specs, out_specs=out_specs, check_vma=False)
```

profile of v0, /device:TPU:8, one launch (start us, length us, event | category | flops | bytes accessed | tf_op | source)
XLA Modules:
  0.0 91.2 jit_solution(2073655433278308061)
XLA Ops:
  0.0 90.3 %shard_map.82 = bf16[128,4096]{1,0:T(8,128)(2,1)S(1)} custom-call(bf16[128,4096]{1,0:T(8,128)(2,1)} %bitcast.12, bf16[128,512]{1,0:T(8,128)(2,1)} %bitcast.14, bf16[128,512]{1,0:T(8,128)(2,1)} %bitcast.15, bf16[128,4096]{1,0:T(8,128)(2,1)} %bitcast.13, s32[1,2048]{1,0:T(1,128)} %doc_ref.1, bf16[256,4096]{1,0:T(8,128)(2,1)} %bitcast.11, ...), custom_call_target="tpu_custom_call" | custom-call | tf_op jit(solution)/shard_map/pallas_call | solution.py:517
  90.3 1.0 %copy.10 = bf16[1,128,4096]{2,1,0:T(8,128)(2,1)} copy(bf16[1,128,4096]{2,1,0:T(8,128)(2,1)S(1)} %bitcast.8) | data formatting | bytes 2097152
where the time goes:
time: 91.4 us; the launch traced here: 91.2 us
  Pallas kernels  90.3 us (99%)
  local copies, waits for them, and re-layouts  0.97 us (1%)
    pallas_call x1, Pallas kernels, body(): pl.pallas_call(kernel, out_shape=pltpu.VMEM((ROWS, D), BF16), in_specs=[h...  90.3 us

commit v1 on v0

--- a/solution.py
+++ b/solution.py
@@ -15,8 +15,11 @@
 CW = D // NC
 W_EARLY = 7
 EARLY = 3
-SLOTS = 8
-ORDER = ('w3', 'p0', 'm0', 'core', 'p3', 'p1', 'm1', 'w4', 'p2', 'p4', 'w5', 'p5', 'm2', 'w6', 'p6', 'ysum', 'm3', 'm4', 'm5', 'dkv', 'w7', 'f0', 'f1', 'f2', 'f3', 'p7', 'm6', 'f4', 'f5', 'm7', 'f6', 'f7')
+SLOTS = 6
+ORDER = (
+    "w3", "core", "p0", "m0", "p3", "p1", "m1", "w4", "p2", "p4", "w5", "p5", "m2", "w6", "p6", "ysum", "m3",
+    "m4", "dkv", "f0", "f1", "m5", "w7", "f2", "f3", "p7", "m6", "f4", "f5", "m7", "f6", "f7",
+)
 WIN = 9
 SCALE = 1.0 / math.sqrt(HD)
 NEG = -1e30
@@ -234,36 +237,12 @@
             half(i, n).start()
         return carry
 
-    def attend(i, carry):
-        d = jnp.where(i == 2, 3, jnp.where(i == 3, 2, i))
-        zb = lax.rem(z + 4 - d, 4)
-        lo, hi = jnp.where(i == 3, 0, 0), jnp.where(i == 3, 3, 0)
-
-        with jax.named_scope("qowait"):
-
-            @pl.when(d == 0)
-            def _():
-                own_q.wait()
-                own_o.wait()
-
-            @pl.when(d > 0)
-            def _():
-                remote(q_ref.at[:, 0:GW], qs.at[zb], qo_s.at[0, d], qo_r.at[0, d], core).wait_recv()
-                remote(o_ref.at[:, 0:GW], os_.at[zb], qo_s.at[1, d], qo_r.at[1, d], core).wait_recv()
-
-        @pl.when(i == 1)
-        def _():
-            own_w.wait()
-            w_core.wait()
-
-        with jax.named_scope("forward"):
-            lax.fori_loop(lo, hi, forward_early, 0)
-        block = zb * 4 + yc
-        at = pl.multiple_of(block * ROWS, ROWS)
-        k_win = kv_rows[pl.ds(at, WIN * ROWS), 0:HD]
-        base = (block - 8) * ROWS
+    def attend_block(zb, at, key_at, win):
+        keys = win * ROWS
+        base = at - 8 * ROWS if win == WIN else 0
         lower = start[:, pl.ds(at, ROWS)] - base
         lower = jnp.concatenate([lower, lower], axis=1)
+        kv_win = pl.ds(key_at, keys)
 
         def heads(hp, carry):
             cols = pl.ds(pl.multiple_of(hp * 2 * HD, 2 * HD), 2 * HD)
@@ -271,24 +250,27 @@
             q2 = jnp.concatenate([q2[:, 0:HD], q2[:, HD:]], axis=0)
             o2 = os_[zb, :, cols]
             o2 = jnp.concatenate([o2[:, 0:HD], o2[:, HD:]], axis=0)
-            v_win = kv_rows[pl.ds(at, WIN * ROWS), HD : 2 * HD]
-            k_win = kv_rows[pl.ds(at, WIN * ROWS), 0:HD]
+            v_win = kv_rows[kv_win, HD : 2 * HD]
+            k_win = kv_rows[kv_win, 0:HD]
             nt = (((1,), (1,)), ((), ()))
             s = lax.dot_general(k_win, q2, nt, preferred_element_type=F32)
-            key = lax.broadcasted_iota(jnp.int32, (8 * ROWS, 2 * ROWS), 0)
-            s_a = jnp.where(key >= lower, s[: 8 * ROWS], NEG)
-            key = lax.broadcasted_iota(jnp.int32, (ROWS, 2 * ROWS), 0)
-            row = lax.broadcasted_iota(jnp.int32, (ROWS, 2 * ROWS), 1)
-            row = jnp.where(row >= ROWS, row - ROWS, row)
-            s_b = jnp.where((key + 8 * ROWS >= lower) & (key <= row), s[8 * ROWS :], NEG)
-            s = jnp.concatenate([s_a, s_b], axis=0)
+            free = 8 * ROWS if win == WIN else 0
+            rest = keys - free
+            key = lax.broadcasted_iota(jnp.int32, (rest, 2 * ROWS), 0) + free
+            row = lax.broadcasted_iota(jnp.int32, (rest, 2 * ROWS), 1)
+            row = jnp.where(row >= ROWS, row - ROWS, row) + (free if win == WIN else yc * ROWS)
+            s_b = jnp.where((key >= lower) & (key <= row), s[free:], NEG)
+            if free:
+                key = lax.broadcasted_iota(jnp.int32, (free, 2 * ROWS), 0)
+                s_b = jnp.concatenate([jnp.where(key >= lower, s[:free], NEG), s_b], axis=0)
+            s = s_b
             top = jnp.max(s, axis=0, keepdims=True)
             e = jnp.exp2((s - top) * (SCALE * math.log2(math.e)))
             inv = 1.0 / jnp.sum(e, axis=0, keepdims=True)
             dp = lax.dot_general(v_win, o2, nt, preferred_element_type=F32)
             delta = jnp.sum(e * dp, axis=0, keepdims=True) * inv
-            p_s[:, cols] = (e * inv).astype(BF16)
-            ds_s[:, cols] = (e * (dp - delta) * (inv * SCALE)).astype(BF16)
+            p_s[0:keys, cols] = (e * inv).astype(BF16)
+            ds_s[0:keys, cols] = (e * (dp - delta) * (inv * SCALE)).astype(BF16)
             return carry
 
         with jax.named_scope("heads"):
@@ -298,14 +280,51 @@
             ob = os_[zb]
             qb = jnp.concatenate([qb[:, h * HD : (h + 1) * HD] for h in range(8)], axis=0)
             ob = jnp.concatenate([ob[:, h * HD : (h + 1) * HD] for h in range(8)], axis=0)
-            win = pl.ds(at, WIN * ROWS)
-            dv[win, :] += jnp.dot(p_s[...], ob, preferred_element_type=F32)
-            dk[win, :] += jnp.dot(ds_s[...], qb, preferred_element_type=F32)
-            dqt = lax.dot_general(k_win, ds_s[...], (((0,), (0,)), ((), ())), preferred_element_type=F32)
+            dv[kv_win, :] += jnp.dot(p_s[0:keys, :], ob, preferred_element_type=F32)
+            dk[kv_win, :] += jnp.dot(ds_s[0:keys, :], qb, preferred_element_type=F32)
+            dqt = lax.dot_general(
+                kv_rows[kv_win, 0:HD], ds_s[0:keys, :], (((0,), (0,)), ((), ())), preferred_element_type=F32
+            )
             for h in range(8):
                 dq[pl.ds(pl.multiple_of(zb * ROWS, ROWS), ROWS), h * HD : (h + 1) * HD] = dqt[
                     :, h * HD : (h + 1) * HD
                 ].T.astype(BF16)
+
+    def attend(i, carry):
+        d = jnp.where(i == 2, 3, jnp.where(i == 3, 2, i))
+        zb = lax.rem(z + 4 - d, 4)
+        lo, hi = jnp.where(i == 3, 0, 0), jnp.where(i == 3, 3, 0)
+
+        with jax.named_scope("qowait"):
+
+            @pl.when(d == 0)
+            def _():
+                own_q.wait()
+                own_o.wait()
+
+            @pl.when(d > 0)
+            def _():
+                remote(q_ref.at[:, 0:GW], qs.at[zb], qo_s.at[0, d], qo_r.at[0, d], core).wait_recv()
+                remote(o_ref.at[:, 0:GW], os_.at[zb], qo_s.at[1, d], qo_r.at[1, d], core).wait_recv()
+
+        @pl.when(i == 1)
+        def _():
+            own_w.wait()
+            w_core.wait()
+
+        with jax.named_scope("forward"):
+            lax.fori_loop(lo, hi, forward_early, 0)
+        block = zb * 4 + yc
+        at = pl.multiple_of(block * ROWS, ROWS)
+
+        @pl.when(zb > 0)
+        def _():
+            attend_block(zb, at, at, WIN)
+
+        @pl.when(zb == 0)
+        def _():
+            attend_block(zb, at, 8 * ROWS, 4)
+
         with jax.named_scope("early"):
             lax.fori_loop(lo, hi, early, 0)
         return carry
@@ -521,7 +540,7 @@
         out_specs=vmem,
         scratch_shapes=scratch,
         compiler_params=pltpu.CompilerParams(
-            collective_id=0, has_side_effects=True, vmem_limit_bytes=60817408
+            collective_id=0, has_side_effects=True, vmem_limit_bytes=62914560
         ),
     )(
         queries[0],

time: 91.4 us -> 90.2 us (0.987)
  Pallas kernels: 90.3 us -> 89.1 us
    pallas_call x1, Pallas kernels: 90.3 us -> 89.1 us  [body(): pl.pallas_call(kernel, out_shape=pltpu.VMEM((ROWS, D), BF16), in_specs=[h...]
where the time goes in v1:
time: 90.2 us; the launch traced here: 90.1 us
  Pallas kernels  89.1 us (99%)
  local copies, waits for them, and re-layouts  0.97 us (1%)
    pallas_call x1, Pallas kernels, body(): pl.pallas_call(kernel, out_shape=pltpu.VMEM((ROWS, D), BF16), in_specs=[h...  89.1 us

profile of v1, /device:TPU:8, one launch (start us, length us, event | category | flops | bytes accessed | tf_op | source)
XLA Modules:
  0.0 90.1 jit_solution(7907808695019671720)
XLA Ops:
  0.0 89.1 %shard_map.82 = bf16[128,4096]{1,0:T(8,128)(2,1)S(1)} custom-call(bf16[128,4096]{1,0:T(8,128)(2,1)} %bitcast.12, bf16[128,512]{1,0:T(8,128)(2,1)} %bitcast.14, bf16[128,512]{1,0:T(8,128)(2,1)} %bitcast.15, bf16[128,4096]{1,0:T(8,128)(2,1)} %bitcast.13, s32[1,2048]{1,0:T(1,128)} %doc_ref.1, bf16[256,4096]{1,0:T(8,128)(2,1)} %bitcast.11, ...), custom_call_target="tpu_custom_call" | custom-call | tf_op jit(solution)/shard_map/pallas_call | solution.py:536
  89.1 1.0 %copy.10 = bf16[1,128,4096]{2,1,0:T(8,128)(2,1)} copy(bf16[1,128,4096]{2,1,0:T(8,128)(2,1)S(1)} %bitcast.8) | data formatting | bytes 2097152

commit v2 on v1

--- a/solution.py
+++ b/solution.py
@@ -17,8 +17,8 @@
 EARLY = 3
 SLOTS = 6
 ORDER = (
-    "w3", "core", "p0", "m0", "p3", "p1", "m1", "w4", "p2", "p4", "w5", "p5", "m2", "w6", "p6", "ysum", "m3",
-    "m4", "dkv", "f0", "f1", "m5", "w7", "f2", "f3", "p7", "m6", "f4", "f5", "m7", "f6", "f7",
+    "w3", "core", "p0", "m0", "p3", "p1", "m1", "w4", "p4", "p2", "w5", "p5", "m2", "w6", "p6", "ysum", "m3",
+    "m4", "dkv", "f0", "f1", "w7", "m5", "f2", "p7", "f3", "m6", "f4", "m7", "f5", "f6", "f7",
 )
 WIN = 9
 SCALE = 1.0 / math.sqrt(HD)

time: 90.2 us -> 90.2 us (level)
  no operation moved by 1% of the time
where the time goes in v2:
time: 90.2 us; the launch traced here: 90.1 us
  Pallas kernels  89.1 us (99%)
  local copies, waits for them, and re-layouts  0.97 us (1%)
    pallas_call x1, Pallas kernels, body(): pl.pallas_call(kernel, out_shape=pltpu.VMEM((ROWS, D), BF16), in_specs=[h...  89.1 us

profile of v2, /device:TPU:8, one launch (start us, length us, event | category | flops | bytes accessed | tf_op | source)
XLA Modules:
  0.0 90.1 jit_solution(3799986711083388021)
XLA Ops:
  0.0 89.1 %shard_map.82 = bf16[128,4096]{1,0:T(8,128)(2,1)S(1)} custom-call(bf16[128,4096]{1,0:T(8,128)(2,1)} %bitcast.12, bf16[128,512]{1,0:T(8,128)(2,1)} %bitcast.14, bf16[128,512]{1,0:T(8,128)(2,1)} %bitcast.15, bf16[128,4096]{1,0:T(8,128)(2,1)} %bitcast.13, s32[1,2048]{1,0:T(1,128)} %doc_ref.1, bf16[256,4096]{1,0:T(8,128)(2,1)} %bitcast.11, ...), custom_call_target="tpu_custom_call" | custom-call | tf_op jit(solution)/shard_map/pallas_call | solution.py:536
  89.1 1.0 %copy.10 = bf16[1,128,4096]{2,1,0:T(8,128)(2,1)} copy(bf16[1,128,4096]{2,1,0:T(8,128)(2,1)S(1)} %bitcast.8) | data formatting | bytes 2097152
